TPU v7x, 32 devices: a whole 2x2x4 slice. The times are simulated.
32 devices in a mesh: dp: 8 (over z, x), tensor: 4 (over y, core).
Axes of the slice: x: 2, y: 2, z: 4, core: 2. Of those that a mesh axis runs over, the one named last changes fastest.
Arguments:
- out_grad: bfloat16 [1536, 2048], P(('dp', 'tensor')), may hold values from -6 to 6
- gate_pre: bfloat16 [1536, 7168], P('dp', 'tensor'), may hold values from -6 to 6
- up_pre: bfloat16 [1536, 7168], P('dp', 'tensor'), may hold values from -6 to 6
- down_weight: bfloat16 [7168, 2048], P('tensor', 'dp'), may hold values from -0.0625 to 0.0625
- up_weight: bfloat16 [2048, 7168], P('dp', 'tensor'), may hold values from -0.125 to 0.125
Outputs:
- input_grad: bfloat16 [1536, 2048], P(('dp', 'tensor'))
- gate_grad: bfloat16 [1536, 7168], P('dp', 'tensor')
- down_grad_t: float32 [2048, 7168], P('dp', 'tensor')
All inputs are finite; a program needn't handle non-finite values.
Results may differ from a plain program's by a relative error of at most 0.009.
Values may be sent and summed in bfloat16 or wider, within the bound.
No kernel may reach another device: no remote copies, remote signals or barrier semaphores. Data moves between devices by JAX's collectives and lax.ppermute only.
A program may use at most 128 MiB of HBM per device.

v0:
```python
import jax
import jax.numpy as jnp
from jax import lax
from jax.sharding import PartitionSpec as P


def shards(out_grad, gate_pre, up_pre, down_weight, up_weight):
    grad_rows = lax.all_gather(out_grad, "tensor", axis=0, tiled=True)
    gate_f = gate_pre.astype(jnp.float32)
    up_f = up_pre.astype(jnp.float32)
    sigmoid_gate = jax.nn.sigmoid(gate_f)
    swish_gate = gate_f * sigmoid_gate
    hidden = (swish_gate * up_f).astype(jnp.bfloat16)
    contract = (((1,), (1,)), ((), ()))
    whole_down, whole_up = (
        lax.all_gather(down_weight, "dp", axis=1, tiled=True),
        lax.all_gather(up_weight, "dp", axis=0, tiled=True),
    )
    upstream = lax.dot_general(grad_rows, whole_down, contract, preferred_element_type=jnp.float32)
    gate_grad = (upstream * up_f * sigmoid_gate * (1.0 + gate_f * (1.0 - sigmoid_gate))).astype(
        jnp.bfloat16
    )
    up_grad = (upstream * swish_gate).astype(jnp.bfloat16)
    replicas = lax.axis_size("dp")
    partial_sum = lax.dot_general(up_grad, whole_up, contract, preferred_element_type=jnp.float32)
    input_grad = lax.psum_scatter(
        partial_sum.astype(jnp.bfloat16), "tensor", scatter_dimension=0, tiled=True
    )
    product = lax.dot_general(
        grad_rows, hidden, (((0,), (0,)), ((), ())), preferred_element_type=jnp.float32
    )
    down_grad = lax.psum_scatter(product / replicas, "dp", scatter_dimension=0, tiled=True)
    return (input_grad, gate_grad, down_grad)


def solution(mesh):
    placed = (
        P(("dp", "tensor"), None),
        P("dp", "tensor"),
        P("dp", "tensor"),
        P("tensor", "dp"),
        P("dp", "tensor"),
    )
    return jax.shard_map(
        shards,
        mesh=mesh,
        in_specs=placed,
        out_specs=(P(("dp", "tensor"), None), P("dp", "tensor"), P("dp", "tensor")),
        check_vma=False,
    )
```

profile of v0, /device:TPU:0, one launch (start us, length us, event | category | flops | bytes accessed | tf_op | source)
XLA Modules:
  0.0 507.6 jit_solution(8489506215518296360)
XLA Ops:
  7.2 0.0 copy-start.2
  7.2 0.0 copy-start.1
  7.2 0.0 copy-start
  7.2 0.0 all-gather.3.cloned.1.call-start
  7.2 0.7 all-gather.3.cloned.1.call-update
  7.9 0.0 all-gather.5.cloned.1.call-start
  8.0 0.7 all-gather.5.cloned.1.call-update
  8.7 0.0 reduce-scatter.5.cloned.1.call-start
  8.7 0.0 copy-done.2
  8.7 10.1 %all_gather.9 = bf16[192,2048]{1,0:T(8,128)(2,1)S(1)} all-gather(bf16[48,2048]{1,0:T(8,128)(2,1)S(1)} %copy-done.2), channel_id=1, replica_groups=mesh['dp'=8,'tensor'=4] {'tensor'}, dimensions={0}, use_global_device_ids=true | all-gather | bytes 983040 | tf_op jit(solution)/shard_map/all_gather | solution.py:8
  18.8 0.0 copy-done.1
  18.8 0.0 copy-done
  18.8 7.4 %multiply_bitcast_fusion = f32[2048,1792]{0,1:T(8,128)} fusion(bf16[192,2048]{1,0:T(8,128)(2,1)S(1)} %all_gather.9, bf16[192,1792]{1,0:T(8,128)(2,1)S(1)} %copy-done, bf16[192,1792]{1,0:T(8,128)(2,1)S(1)} %copy-done.1), kind=kOutput, calls=%fused_computation | convolution fusion | flops 1415708672 | bytes 16842752 | tf_op jit(solution)/shard_map/dot_general | solution.py:29
  26.2 0.0 reduce-scatter.5.cloned.1.call-update
  26.2 0.0 reduce-scatter.3.cloned.1.call-start
  26.3 98.7 %all-gather.3.cloned.1.call-done = bf16[1792,2048]{1,0:T(8,128)(2,1)} async-done(((bf16[1792,256]{1,0:T(8,128)(2,1)}), bf16[1792,2048]{1,0:T(8,128)(2,1)}) %all-gather.3.cloned.1.call-update) | async-done | bytes 7340048 | tf_op jit(solution)/shard_map/all_gather | solution.py:16
  125.0 7.1 %fusion.2 = (bf16[192,1792]{1,0:T(8,128)(2,1)}, f32[192,1792]{1,0:T(8,128)}) fusion(bf16[192,1792]{1,0:T(8,128)(2,1)S(1)} %copy-done, bf16[192,1792]{1,0:T(8,128)(2,1)S(1)} %copy-done.1, bf16[192,2048]{1,0:T(8,128)(2,1)S(1)} %all_gather.9, bf16[1792,2048]{1,0:T(8,128)(2,1)} %all-gather.3.cloned.1.call-done), kind=kOutput, calls=%fused_computation.9 | convolution fusion | flops 1413414912 | bytes 11567104 | tf_op jit(solution)/shard_map/dot_general | solution.py:19
  132.1 104.8 %all-gather.5.cloned.1.call-done = bf16[2048,1792]{1,0:T(8,128)(2,1)} async-done(((bf16[256,1792]{1,0:T(8,128)(2,1)}), bf16[2048,1792]{1,0:T(8,128)(2,1)}) %all-gather.5.cloned.1.call-update) | async-done | bytes 7340048 | tf_op jit(solution)/shard_map/all_gather | solution.py:17
  236.9 7.0 %convolution_convert_fusion = bf16[192,2048]{1,0:T(8,128)(2,1)} fusion(bf16[2048,1792]{1,0:T(8,128)(2,1)} %all-gather.5.cloned.1.call-done, f32[192,1792]{1,0:T(8,128)} %get-tuple-element.7, bf16[192,1792]{1,0:T(8,128)(2,1)S(1)} %copy-done.1), kind=kOutput, calls=%fused_computation.1 | convolution fusion | flops 1412087808 | bytes 10190848 | tf_op jit(solution)/shard_map/dot_general | solution.py:25
  243.8 0.0 reduce-scatter.3.cloned.1.call-update
  243.8 231.9 %reduce-scatter.5.cloned.1.call-done = f32[256,1792]{0,1:T(8,128)} async-done(((f32[2048,1792]{0,1:T(8,128)}), f32[256,1792]{0,1:T(8,128)}) %reduce-scatter.5.cloned.1.call-update) | async-done | bytes 1835024 | tf_op jit(solution)/shard_map/reduce_scatter | solution.py:32
  475.7 2.7 copy.8
  478.5 22.6 %reduce-scatter.3.cloned.1.call-done = bf16[48,2048]{1,0:T(8,128)(2,1)} async-done(((bf16[192,2048]{1,0:T(8,128)(2,1)}), bf16[48,2048]{1,0:T(8,128)(2,1)}) %reduce-scatter.3.cloned.1.call-update) | async-done | bytes 196624 | tf_op jit(solution)/shard_map/reduce_scatter | solution.py:26
Async XLA Ops:
  7.2 1.6 copy-start.2
  7.2 11.7 %copy-start.1 = (bf16[192,1792]{1,0:T(8,128)(2,1)S(1)}, bf16[192,1792]{1,0:T(8,128)(2,1)}, u32[]{:S(2)}) copy-start(bf16[192,1792]{1,0:T(8,128)(2,1)} %param.6) | copy-start | bytes 2064388
  7.2 11.7 %copy-start = (bf16[192,1792]{1,0:T(8,128)(2,1)S(1)}, bf16[192,1792]{1,0:T(8,128)(2,1)}, u32[]{:S(2)}) copy-start(bf16[192,1792]{1,0:T(8,128)(2,1)} %param.7) | copy-start | bytes 2064388
  7.2 117.8 %all-gather.3.cloned.1.call-start = ((), (), s32[]{:S(2)}) async-start(), calls=%async_computation.2 | async-start | bytes 8257536 | tf_op jit(solution)/shard_map/all_gather | solution.py:16
  7.9 228.9 %all-gather.5.cloned.1.call-start = ((), (), s32[]{:S(2)}) async-start(), calls=%async_computation.3 | async-start | bytes 8257536 | tf_op jit(solution)/shard_map/all_gather | solution.py:17
  8.7 467.1 %reduce-scatter.5.cloned.1.call-start = ((), (), s32[]{:S(2)}) async-start(), calls=%async_computation.5 | async-start | bytes 16515072 | tf_op jit(solution)/shard_map/reduce_scatter | solution.py:32
  26.2 474.8 %reduce-scatter.3.cloned.1.call-start = ((), (), s32[]{:S(2)}) async-start(), calls=%async_computation.4 | async-start | bytes 983040 | tf_op jit(solution)/shard_map/reduce_scatter | solution.py:26
Sparse Core Ops, SparseCore 0:
  10.0 114.8 all-gather.2
  127.2 109.6 all-gather.4
  240.5 235.2 reduce-scatter.4
  478.7 22.3 reduce-scatter.2
where the time goes:
time: 508 us
  waiting for transfers between devices  459 us (90%)
  matrix products  21.5 us (4%)
  between operations  13.8 us (3%)
  blocking collectives  10.1 us (2%)
    reduce_scatter x1, waiting for transfers between devices, shards(): lax.psum_scatter(product / replicas, 'dp', scatter_dimension=0, tiled=True)  232 us
    all_gather x1, waiting for transfers between devices, shards(): lax.all_gather(up_weight, 'dp', axis=0, tiled=True)  105 us
    all_gather x1, waiting for transfers between devices, shards(): lax.all_gather(down_weight, 'dp', axis=1, tiled=True)  98.7 us
    reduce_scatter x1, waiting for transfers between devices, shards(): lax.psum_scatter(partial_sum.astype(jnp.bfloat16), 'tensor', scatter_dime...  22.6 us
  transfers between devices with their start and end apart: 4, of which 4 were waited for; matrix products, arithmetic and copies ran while one was open for 5% of the time, Pallas kernels for 0%

commit v1 on v0

--- a/solution.py
+++ b/solution.py
@@ -14,7 +14,9 @@
     contract = (((1,), (1,)), ((), ()))
     whole_down, whole_up = (
         lax.all_gather(down_weight, "dp", axis=1, tiled=True),
-        lax.all_gather(up_weight, "dp", axis=0, tiled=True),
+        jnp.concatenate(
+            lax.all_to_all(jnp.stack([up_weight] * lax.axis_size("dp")), "dp", 0, 0), axis=0
+        ),
     )
     upstream = lax.dot_general(grad_rows, whole_down, contract, preferred_element_type=jnp.float32)
     gate_grad = (upstream * up_f * sigmoid_gate * (1.0 + gate_f * (1.0 - sigmoid_gate))).astype(

time: 508 us -> 533 us (1.049)
  waiting for transfers between devices: 459 us -> 475 us
  starting transfers between devices: 0.16 us -> 5.95 us
    all_gather x1, waiting for transfers between devices: 98.7 us -> 224 us  [shards(): lax.all_gather(down_weight, 'dp', axis=1, tiled=True)]
    all_gather x1 -> x0, waiting for transfers between devices: 105 us -> none  [shards(): lax.all_gather(up_weight, 'dp', axis=0, tiled=True)]
    reduce_scatter x1, waiting for transfers between devices: 232 us -> 214 us  [shards(): lax.psum_scatter(product / replicas, 'dp', scatter_dimension=0, tiled=True)]
    all_to_all x0 -> x1, waiting for transfers between devices: none -> 14.1 us  [shards(): lax.all_to_all(jnp.stack([up_weight] * lax.axis_size('dp')), 'dp', 0, 0)]
    all_to_all x0 -> x1, starting transfers between devices: none -> 5.83 us  [shards(): lax.all_to_all(jnp.stack([up_weight] * lax.axis_size('dp')), 'dp', 0, 0)]
where the time goes in v1:
time: 533 us
  waiting for transfers between devices  475 us (89%)
  matrix products  20.8 us (4%)
  between operations  13.8 us (3%)
  blocking collectives  10.3 us (2%)
  local copies, waits for them, and re-layouts  7.34 us (1%)
  starting transfers between devices  5.95 us (1%)
    all_gather x1, waiting for transfers between devices, shards(): lax.all_gather(down_weight, 'dp', axis=1, tiled=True)  224 us
    reduce_scatter x1, waiting for transfers between devices, shards(): lax.psum_scatter(product / replicas, 'dp', scatter_dimension=0, tiled=True)  214 us
    reduce_scatter x1, waiting for transfers between devices, shards(): lax.psum_scatter(partial_sum.astype(jnp.bfloat16), 'tensor', scatter_dime...  22.7 us
    all_to_all x1, waiting for transfers between devices, shards(): lax.all_to_all(jnp.stack([up_weight] * lax.axis_size('dp')), 'dp', 0, 0)  14.1 us
  transfers between devices with their start and end apart: 4, of which 4 were waited for; matrix products, arithmetic and copies ran while one was open for 5% of the time, Pallas kernels for 0%

profile of v1, /device:TPU:0, one launch (start us, length us, event | category | flops | bytes accessed | tf_op | source)
XLA Modules:
  0.0 532.9 jit_solution(7501408144461446690)
XLA Ops:
  7.2 0.0 copy-start.1
  7.2 0.0 copy-start.2
  7.2 0.0 all-gather.2.cloned.1.call-start
  7.2 0.7 all-gather.2.cloned.1.call-update
  7.9 0.0 reduce-scatter.5.cloned.1.call-start
  8.0 10.3 %all_gather.6 = bf16[192,2048]{1,0:T(8,128)(2,1)S(1)} all-gather(bf16[48,2048]{1,0:T(8,128)(2,1)} %param.5), channel_id=1, replica_groups=mesh['dp'=8,'tensor'=4] {'tensor'}, dimensions={0}, use_global_device_ids=true | all-gather | bytes 983040 | tf_op jit(solution)/shard_map/all_gather | solution.py:8
  18.3 0.0 copy-done.1
  18.3 0.0 copy-done.2
  18.3 7.5 %multiply_bitcast_fusion = f32[2048,1792]{0,1:T(8,128)} fusion(bf16[192,2048]{1,0:T(8,128)(2,1)S(1)} %all_gather.6, bf16[192,1792]{1,0:T(8,128)(2,1)S(1)} %copy-done.1, bf16[192,1792]{1,0:T(8,128)(2,1)S(1)} %copy-done.2), kind=kOutput, calls=%fused_computation | convolution fusion | flops 1415708672 | bytes 16842752 | tf_op jit(solution)/shard_map/dot_general | solution.py:31
  25.8 0.0 copy-start
  25.8 0.0 reduce-scatter.5.cloned.1.call-update
  25.8 1.2 copy-done
  27.0 3.5 stack.2
  30.4 5.8 %all-to-all-start = ((bf16[8,256,1792]{2,1,0:T(8,128)(2,1)}), bf16[8,256,1792]{2,1,0:T(8,128)(2,1)}, u32[]{:S(2)}, u32[]{:S(2)}) async-start(bf16[8,256,1792]{2,1,0:T(8,128)(2,1)} %stack.2), calls=%async_computation | async-start | bytes 14680064 | tf_op jit(solution)/shard_map/all_to_all | solution.py:18
  36.3 0.0 reduce-scatter.3.cloned.1.call-start
  36.3 223.7 %all-gather.2.cloned.1.call-done = bf16[1792,2048]{1,0:T(8,128)(2,1)} async-done(((bf16[1792,256]{1,0:T(8,128)(2,1)}), bf16[1792,2048]{1,0:T(8,128)(2,1)}) %all-gather.2.cloned.1.call-update) | async-done | bytes 7340048 | tf_op jit(solution)/shard_map/all_gather | solution.py:16
  260.0 6.7 %fusion.2 = (bf16[192,1792]{1,0:T(8,128)(2,1)}, f32[192,1792]{1,0:T(8,128)S(1)}) fusion(bf16[192,1792]{1,0:T(8,128)(2,1)S(1)} %copy-done.1, bf16[192,1792]{1,0:T(8,128)(2,1)S(1)} %copy-done.2, bf16[192,2048]{1,0:T(8,128)(2,1)S(1)} %all_gather.6, bf16[1792,2048]{1,0:T(8,128)(2,1)} %all-gather.2.cloned.1.call-done), kind=kOutput, calls=%fused_computation.9 | convolution fusion | flops 1413414912 | bytes 11567104 | tf_op jit(solution)/shard_map/dot_general | solution.py:21
  266.8 14.1 %all-to-all-done = bf16[8,256,1792]{2,1,0:T(8,128)(2,1)} async-done(((bf16[8,256,1792]{2,1,0:T(8,128)(2,1)}), bf16[8,256,1792]{2,1,0:T(8,128)(2,1)}, u32[]{:S(2)}, u32[]{:S(2)}) %all-to-all-start) | async-done | bytes 7340064 | tf_op jit(solution)/shard_map/all_to_all | solution.py:18
  280.8 6.6 %convolution_convert_fusion = bf16[192,2048]{1,0:T(8,128)(2,1)} fusion(bf16[2048,1792]{1,0:T(8,128)(2,1)} %bitcast, f32[192,1792]{1,0:T(8,128)S(1)} %get-tuple-element.7, bf16[192,1792]{1,0:T(8,128)(2,1)S(1)} %copy-done.2), kind=kOutput, calls=%fused_computation.1 | convolution fusion | flops 1412087808 | bytes 10190848 | tf_op jit(solution)/shard_map/dot_general | solution.py:27
  287.4 0.0 reduce-scatter.3.cloned.1.call-update
  287.5 213.5 %reduce-scatter.5.cloned.1.call-done = f32[256,1792]{0,1:T(8,128)} async-done(((f32[2048,1792]{0,1:T(8,128)}), f32[256,1792]{0,1:T(8,128)}) %reduce-scatter.5.cloned.1.call-update) | async-done | bytes 1835024 | tf_op jit(solution)/shard_map/reduce_scatter | solution.py:34
  501.0 2.7 copy.8
  503.7 22.7 %reduce-scatter.3.cloned.1.call-done = bf16[48,2048]{1,0:T(8,128)(2,1)} async-done(((bf16[192,2048]{1,0:T(8,128)(2,1)}), bf16[48,2048]{1,0:T(8,128)(2,1)}) %reduce-scatter.3.cloned.1.call-update) | async-done | bytes 196624 | tf_op jit(solution)/shard_map/reduce_scatter | solution.py:28
Async XLA Ops:
  7.2 11.1 %copy-start.1 = (bf16[192,1792]{1,0:T(8,128)(2,1)S(1)}, bf16[192,1792]{1,0:T(8,128)(2,1)}, u32[]{:S(2)}) copy-start(bf16[192,1792]{1,0:T(8,128)(2,1)} %param.7) | copy-start | bytes 2064388
  7.2 11.1 %copy-start.2 = (bf16[192,1792]{1,0:T(8,128)(2,1)S(1)}, bf16[192,1792]{1,0:T(8,128)(2,1)}, u32[]{:S(2)}) copy-start(bf16[192,1792]{1,0:T(8,128)(2,1)} %param.6) | copy-start | bytes 2064388
  7.2 252.9 %all-gather.2.cloned.1.call-start = ((), (), s32[]{:S(2)}) async-start(), calls=%async_computation.3 | async-start | bytes 8257536 | tf_op jit(solution)/shard_map/all_gather | solution.py:16
  7.9 493.0 %reduce-scatter.5.cloned.1.call-start = ((), (), s32[]{:S(2)}) async-start(), calls=%async_computation.5 | async-start | bytes 16515072 | tf_op jit(solution)/shard_map/reduce_scatter | solution.py:34
  25.8 1.2 copy-start
  30.4 250.4 %all-to-all-start = ((bf16[8,256,1792]{2,1,0:T(8,128)(2,1)}), bf16[8,256,1792]{2,1,0:T(8,128)(2,1)}, u32[]{:S(2)}, u32[]{:S(2)}) async-start(bf16[8,256,1792]{2,1,0:T(8,128)(2,1)} %stack.2), calls=%async_computation | async-start | bytes 14680064 | tf_op jit(solution)/shard_map/all_to_all | solution.py:18
  36.3 490.1 %reduce-scatter.3.cloned.1.call-start = ((), (), s32[]{:S(2)}) async-start(), calls=%async_computation.4 | async-start | bytes 983040 | tf_op jit(solution)/shard_map/reduce_scatter | solution.py:28
Sparse Core Ops, SparseCore 0:
  10.0 249.9 all-gather.1
  263.6 237.2 reduce-scatter.4
  504.1 22.2 reduce-scatter.2
